TPU v7x, 32 devices: a whole 2x2x4 slice. The times are simulated.
32 devices in a mesh: seq: 2 (over x), tensor: 4 (over z), bucket: 4 (over y, core).
Axes of the slice: x: 2, y: 2, z: 4, core: 2. Of those that a mesh axis runs over, the one named last changes fastest.
Arguments:
- queries: bfloat16 [4, 1024, 3072], P('bucket', ('seq', 'tensor')), may hold values from -6 to 6
- keys: bfloat16 [4, 1024, 3072], P('bucket', ('seq', 'tensor')), may hold values from -6 to 6
- values: bfloat16 [4, 1024, 3072], P('bucket', ('seq', 'tensor')), may hold values from -6 to 6
- lengths: int32 [4], P('bucket'), may hold values from 256 to 1024, as said below
- out_weight: bfloat16 [3072, 3072], P(('seq', 'bucket'), 'tensor'), may hold values from -0.109375 to 0.109375
Outputs:
- projected: bfloat16 [4, 1024, 3072], P('bucket', ('seq', 'tensor'))
Inputs may be any that keep to these rules, and one draw needn't show every extreme that they name: `lengths`: each bucket has 256 to 1024 live tokens, and at least one bucket has all 1024.
All inputs are finite; a program needn't handle non-finite values.
Results may differ from a plain program's by a relative error of at most 0.018.
Values may be sent and summed in bfloat16 or wider, within the bound.
No kernel may reach another device: no remote copies, remote signals or barrier semaphores. Data moves between devices by JAX's collectives and lax.ppermute only.
A program may use at most 128 MiB of HBM per device.

v0:
```python
import jax
import jax.numpy as jnp
from jax import lax
from jax.sharding import PartitionSpec as P

HS = 128
MASKED_SCORE = -1e30


def shards(queries, keys, values, lengths, out_weight):
    tok_rows = queries.shape[1]
    n_tensor = lax.axis_size("tensor")
    tensor_index = lax.axis_index("tensor")
    live_len = lengths[0]
    local_q, local_k, local_v = (
        lax.all_to_all(queries[0], "seq", split_axis=1, concat_axis=0, tiled=True),
        lax.all_to_all(keys[0], "seq", split_axis=1, concat_axis=0, tiled=True),
        lax.all_to_all(values[0], "seq", split_axis=1, concat_axis=0, tiled=True),
    )
    row_count, col_count = local_q.shape
    head_count = col_count // HS
    query_heads = local_q.reshape(row_count, head_count, HS)

    def spots(first_row, total_rows):
        index_row = first_row + jnp.arange(total_rows, dtype=jnp.int32)
        owner = index_row // row_count
        within = index_row % row_count
        return (within // tok_rows * n_tensor + owner) * tok_rows + within % tok_rows

    query_usable = spots(tensor_index * row_count, row_count) < live_len
    initial = (
        jnp.full((row_count, head_count), MASKED_SCORE, jnp.float32),
        jnp.zeros((row_count, head_count), jnp.float32),
        jnp.zeros((row_count, head_count, HS), jnp.float32),
    )
    carried = initial
    first_row = jnp.int32(0)
    key_rows = lax.all_gather(local_k, "tensor", axis=0, tiled=True)
    value_rows = lax.all_gather(local_v, "tensor", axis=0, tiled=True)
    for offset in range(key_rows.shape[0] // row_count):
        row_peak, row_sum, accumulated = carried
        key_tile = key_rows[offset * row_count : (offset + 1) * row_count].reshape(
            row_count, head_count, HS
        )
        value_tile = value_rows[offset * row_count : (offset + 1) * row_count].reshape(
            row_count, head_count, HS
        )
        key_usable = spots(first_row + offset * row_count, row_count) < live_len
        scores = jnp.einsum(
            "qhd,khd->qhk", query_heads, key_tile, preferred_element_type=jnp.float32
        ) * HS ** (-0.5)
        scores = jnp.where(key_usable[None, None, :], scores, MASKED_SCORE)
        peak_new = jnp.maximum(row_peak, jnp.max(scores, axis=-1))
        exponent = jnp.where(key_usable[None, None, :], jnp.exp(scores - peak_new[..., None]), 0.0)
        rescale = jnp.exp(row_peak - peak_new)
        accumulated = accumulated * rescale[..., None] + jnp.einsum(
            "qhk,khd->qhd",
            exponent.astype(jnp.bfloat16),
            value_tile,
            preferred_element_type=jnp.float32,
        )
        carried = (peak_new, row_sum * rescale + jnp.sum(exponent, axis=-1), accumulated)
    row_peak, row_sum, accumulated = carried
    attended = accumulated / row_sum[..., None]
    mixed = jnp.where(query_usable[:, None], attended.reshape(row_count, col_count), 0.0).astype(
        jnp.bfloat16
    )
    restored = lax.all_to_all(mixed, "seq", split_axis=0, concat_axis=1, tiled=True)
    wide_weight = lax.all_gather(out_weight, "tensor", axis=1, tiled=True)
    summed = jnp.dot(
        restored,
        lax.all_gather(wide_weight, ("seq", "bucket"), axis=0, tiled=True),
        preferred_element_type=jnp.float32,
    )
    return summed.astype(jnp.bfloat16)[None]


def solution(mesh):
    in_specs = (
        P("bucket", ("seq", "tensor"), None),
        P("bucket", ("seq", "tensor"), None),
        P("bucket", ("seq", "tensor"), None),
        P("bucket"),
        P(("seq", "bucket"), "tensor"),
    )
    out_specs = P("bucket", ("seq", "tensor"), None)
    return jax.shard_map(shards, mesh=mesh, in_specs=in_specs, out_specs=out_specs, check_vma=False)
```

profile of v0, /device:TPU:0, one launch (start us, length us, event | category | flops | bytes accessed | tf_op | source)
XLA Modules:
  0.0 309.9 jit_solution(5005568359367810147)
XLA Ops:
  6.5 0.0 copy-start
  6.5 0.0 all-gather.9.cloned.1.call-start
  6.5 0.7 all-gather.9.cloned.1.call-update
  7.3 0.0 all-gather.5.cloned.1.call-start
  7.3 1.5 copy.68
  8.8 14.8 %all_to_all.70 = bf16[128,2,1536]{0,2,1:T(8,128)(2,1)S(1)} all-to-all(bf16[128,2,1536]{0,2,1:T(8,128)(2,1)S(1)} %bitcast.125), channel_id=1, replica_groups=mesh['seq'=2,'tensor'=4,'bucket'=4] {'seq'}, dimensions={1} | all-to-all | bytes 1572864 | tf_op jit(solution)/shard_map/all_to_all | solution.py:17
  23.6 1.2 copy.69
  24.8 0.0 all-gather.5.cloned.1.call-update
  24.8 0.0 all-gather.7.cloned.1.call-start
  24.9 0.0 copy-done
  24.9 0.4 copy.75
  25.3 0.0 copy-start.1
  25.3 12.5 %all_to_all.71 = bf16[128,2,1536]{0,2,1:T(8,128)(2,1)S(1)} all-to-all(bf16[128,2,1536]{0,2,1:T(8,128)(2,1)S(1)} %bitcast.126), channel_id=1, replica_groups=mesh['seq'=2,'tensor'=4,'bucket'=4] {'seq'}, dimensions={1} | all-to-all | bytes 1572864 | tf_op jit(solution)/shard_map/all_to_all | solution.py:18
  37.8 1.2 copy.76
  38.9 0.0 all-gather.7.cloned.1.call-update
  39.0 0.0 all-gather.11.cloned.1.call-start
  39.0 22.6 %all-gather.9.cloned.1.call-done = bf16[384,3072]{1,0:T(8,128)(2,1)} async-done(((bf16[384,768]{1,0:T(8,128)(2,1)}), bf16[384,3072]{1,0:T(8,128)(2,1)}) %all-gather.9.cloned.1.call-update) | async-done | bytes 2359312 | tf_op jit(solution)/shard_map/all_gather | solution.py:69
  61.6 0.0 all-gather.11.cloned.1.call-update
  61.7 0.0 copy-done.1
  61.7 1.2 copy.71
  62.8 3.5 %all-to-all-start.1 = ((bf16[128,2,1536]{0,2,1:T(8,128)(2,1)}), bf16[128,2,1536]{0,2,1:T(8,128)(2,1)S(1)}, u32[]{:S(2)}, u32[]{:S(2)}) async-start(bf16[128,2,1536]{0,2,1:T(8,128)(2,1)} %bitcast.5), calls=%async_computation.1 | async-start | bytes 1572864 | tf_op jit(solution)/shard_map/all_to_all | solution.py:16
  67.1 10.2 %all-to-all-done.1 = bf16[128,2,1536]{0,2,1:T(8,128)(2,1)S(1)} async-done(((bf16[128,2,1536]{0,2,1:T(8,128)(2,1)}), bf16[128,2,1536]{0,2,1:T(8,128)(2,1)S(1)}, u32[]{:S(2)}, u32[]{:S(2)}) %all-to-all-start.1) | async-done | bytes 786464 | tf_op jit(solution)/shard_map/all_to_all | solution.py:16
  77.3 6.7 %copy.72 = bf16[2,128,1536]{1,0,2:T(2,128)(2,1)S(1)} copy(bf16[2,128,1536]{1,2,0:T(8,128)(2,1)S(1)} %bitcast.122) | data formatting | bytes 1572864 | tf_op jit(solution)/shard_map/all_to_all | solution.py:16
  83.9 0.5 reshape.424
  84.4 41.0 %all-gather.5.cloned.1.call-done = bf16[1024,1536]{1,0:T(8,128)(2,1)} async-done(((bf16[256,1536]{1,0:T(8,128)(2,1)}), bf16[1024,1536]{1,0:T(8,128)(2,1)}) %all-gather.5.cloned.1.call-update) | async-done | bytes 3145744 | tf_op jit(solution)/shard_map/all_gather | solution.py:38
  125.4 2.9 fusion.89
  128.4 1.2 copy.70
  129.6 0.3 copy.92
  129.8 0.3 copy.86
  130.1 1.4 copy.80
  131.5 57.6 %all-gather.7.cloned.1.call-done = bf16[1024,1536]{1,0:T(8,128)(2,1)} async-done(((bf16[256,1536]{1,0:T(8,128)(2,1)}), bf16[1024,1536]{1,0:T(8,128)(2,1)}) %all-gather.7.cloned.1.call-update) | async-done | bytes 3145744 | tf_op jit(solution)/shard_map/all_gather | solution.py:39
  189.1 3.6 %fusion.88 = (bf16[256,1536]{1,0:T(8,128)(2,1)}, bf16[256,1536]{1,0:T(8,128)(2,1)}, bf16[256,1536]{1,0:T(8,128)(2,1)}, bf16[256,1536]{1,0:T(8,128)(2,1)}) fusion(bf16[1024,1536]{1,0:T(8,128)(2,1)} %all-gather.7.cloned.1.call-done), kind=kLoop, calls=%fused_computation.155 | loop fusion | bytes 6291456 | tf_op jit(solution)/shard_map/slice | solution.py:45
  192.7 2.3 copy.83
  195.0 2.5 copy.89
  197.5 2.4 copy.95
  199.9 2.5 copy.77
  202.4 1.9 bitcast_reduce_fusion.3
  204.3 0.8 bitcast_reduce_fusion
  205.2 0.8 bitcast_reduce_fusion.1
  206.1 0.8 bitcast_reduce_fusion.2
  206.9 0.8 fusion.11
  207.8 0.8 fusion.13
  208.6 0.0 copy-start.5
  208.6 0.8 fusion.15
  209.5 0.8 fusion.9
  210.4 0.0 copy-done.5
  210.4 0.0 copy-start.4
  210.4 1.2 fusion.21
  211.5 0.0 copy-done.4
  211.6 0.0 copy-start.3
  211.6 1.4 fusion.19
  212.9 0.0 copy-done.3
  212.9 0.0 copy-start.2
  212.9 1.2 fusion.17
  214.2 0.0 copy-done.2
  214.2 3.0 fusion.25
  217.2 0.3 copy.98
  217.5 0.2 reshape.432
  217.7 0.8 select_convert_fusion
  218.4 0.1 copy.99
  218.6 16.7 %all_to_all.72 = bf16[2,128,1536]{1,2,0:T(8,128)(2,1)S(1)} all-to-all(bf16[2,128,1536]{1,2,0:T(8,128)(2,1)S(1)} %copy.99), channel_id=1, replica_groups=mesh['seq'=2,'tensor'=4,'bucket'=4] {'seq'}, dimensions={0} | all-to-all | bytes 1572864 | tf_op jit(solution)/shard_map/all_to_all | solution.py:68
  235.3 58.3 %all-gather.11.cloned.1.call-done = bf16[3072,3072]{1,0:T(8,128)(2,1)} async-done(((bf16[384,3072]{1,0:T(8,128)(2,1)}), bf16[3072,3072]{1,0:T(8,128)(2,1)}) %all-gather.11.cloned.1.call-update) | async-done | bytes 18874384 | tf_op jit(solution)/shard_map/all_gather | solution.py:72
  293.5 9.9 %fusion = bf16[1,128,3072]{2,1,0:T(8,128)(2,1)} fusion(bf16[128,3072]{0,1:T(8,128)(2,1)S(1)} %bitcast.115, bf16[3072,3072]{1,0:T(8,128)(2,1)} %all-gather.11.cloned.1.call-done), kind=kOutput, calls=%fused_computation.1 | convolution fusion | flops 2416312320 | bytes 20447232 | tf_op jit(solution)/shard_map/dot_general | solution.py:70
  (5 shorter events, 0.1 us)
Async XLA Ops:
  6.5 18.3 %copy-start = (bf16[1,128,3072]{2,1,0:T(8,128)(2,1)S(1)}, bf16[1,128,3072]{2,1,0:T(8,128)(2,1)}, u32[]{:S(2)}) copy-start(bf16[1,128,3072]{2,1,0:T(8,128)(2,1)} %param.7) | copy-start | bytes 2359300
  6.5 55.1 %all-gather.9.cloned.1.call-start = ((), (), s32[]{:S(2)}) async-start(), calls=%async_computation.6 | async-start | bytes 2949120 | tf_op jit(solution)/shard_map/all_gather | solution.py:69
  7.3 118.2 %all-gather.5.cloned.1.call-start = ((), (), s32[]{:S(2)}) async-start(), calls=%async_computation.4 | async-start | bytes 3932160 | tf_op jit(solution)/shard_map/all_gather | solution.py:38
  24.8 164.3 %all-gather.7.cloned.1.call-start = ((), (), s32[]{:S(2)}) async-start(), calls=%async_computation.5 | async-start | bytes 3932160 | tf_op jit(solution)/shard_map/all_gather | solution.py:39
  25.3 36.4 %copy-start.1 = (bf16[1,128,3072]{2,1,0:T(8,128)(2,1)S(1)}, bf16[1,128,3072]{2,1,0:T(8,128)(2,1)}, u32[]{:S(2)}) copy-start(bf16[1,128,3072]{2,1,0:T(8,128)(2,1)} %param.5) | copy-start | bytes 2359300
  39.0 254.6 %all-gather.11.cloned.1.call-start = ((), (), s32[]{:S(2)}) async-start(), calls=%async_computation.7 | async-start | bytes 21233664 | tf_op jit(solution)/shard_map/all_gather | solution.py:72
  62.8 14.4 %all-to-all-start.1 = ((bf16[128,2,1536]{0,2,1:T(8,128)(2,1)}), bf16[128,2,1536]{0,2,1:T(8,128)(2,1)S(1)}, u32[]{:S(2)}, u32[]{:S(2)}) async-start(bf16[128,2,1536]{0,2,1:T(8,128)(2,1)} %bitcast.5), calls=%async_computation.1 | async-start | bytes 1572864 | tf_op jit(solution)/shard_map/all_to_all | solution.py:16
  208.6 1.7 copy-start.5
  210.4 1.2 copy-start.4
  211.6 1.4 copy-start.3
  212.9 1.2 copy-start.2
Sparse Core Ops, SparseCore 0:
  8.9 52.6 all-gather.8
  63.2 62.1 all-gather.4
  127.0 62.0 all-gather.6
  190.9 102.6 all-gather.10
where the time goes:
time: 311 us; the launch traced here: 310 us
  waiting for transfers between devices  190 us (61%)
  blocking collectives  44 us (14%)
  local copies, waits for them, and re-layouts  32.5 us (10%)
  matrix products  21.1 us (7%)
  between operations  14.1 us (5%)
  other arithmetic  4.22 us (1%)
  starting transfers between devices  3.66 us (1%)
    all_gather x1, waiting for transfers between devices, shards(): lax.all_gather(wide_weight, ('seq', 'bucket'), axis=0, tiled=True)  58.3 us
    all_gather x1, waiting for transfers between devices, shards(): value_rows = lax.all_gather(local_v, 'tensor', axis=0, tiled=True)  57.6 us
    all_gather x1, waiting for transfers between devices, shards(): key_rows = lax.all_gather(local_k, 'tensor', axis=0, tiled=True)  41 us
    all_gather x1, waiting for transfers between devices, shards(): wide_weight = lax.all_gather(out_weight, 'tensor', axis=1, tiled=True)  22.6 us
    all_to_all x1, blocking collectives, shards(): lax.all_to_all(mixed, 'seq', split_axis=0, concat_axis=1, tiled=True)  16.7 us
    all_to_all x1, blocking collectives, shards(): lax.all_to_all(keys[0], 'seq', split_axis=1, concat_axis=0, tiled=True)  14.8 us
    slice x5, local copies, waits for them, and re-layouts, shards(): value_rows[offset * row_count:(offset + 1) * row_count]  13.3 us
    all_to_all x1, blocking collectives, shards(): lax.all_to_all(values[0], 'seq', split_axis=1, concat_axis=0, tiled=True)  12.5 us
  transfers between devices with their start and end apart: 5, of which 5 were waited for; matrix products, arithmetic and copies ran while one was open for 15% of the time, Pallas kernels for 0%

commit v1 on v0

--- a/solution.py
+++ b/solution.py
@@ -35,8 +35,11 @@
     )
     carried = initial
     first_row = jnp.int32(0)
-    key_rows = lax.all_gather(local_k, "tensor", axis=0, tiled=True)
-    value_rows = lax.all_gather(local_v, "tensor", axis=0, tiled=True)
+    key_rows, value_rows = jnp.split(
+        lax.all_gather(jnp.concatenate([local_k, local_v], axis=1), "tensor", axis=0, tiled=True),
+        [local_k.shape[1]],
+        axis=1,
+    )
     for offset in range(key_rows.shape[0] // row_count):
         row_peak, row_sum, accumulated = carried
         key_tile = key_rows[offset * row_count : (offset + 1) * row_count].reshape(

time: 311 us -> 300 us (0.965)
  waiting for transfers between devices: 190 us -> 214 us
  blocking collectives: 44 us -> 22.8 us
  local copies, waits for them, and re-layouts: 32.5 us -> 15.4 us
  starting transfers between devices: 3.66 us -> 11.4 us
  matrix products: 21.1 us -> 17.3 us
    all_to_all x2 -> x0, blocking collectives: 27.3 us -> none  [the longest x1 14.8 us: shards(): lax.all_to_all(keys[0], 'seq', split_axis=1, concat_axis=0, tiled=True)]
    all_to_all x0 -> x2, waiting for transfers between devices: none -> 20.9 us  [the longest x1 10.4 us: shards(): lax.all_to_all(keys[0], 'seq', split_axis=1, concat_axis=0, tiled=True)]
    all_gather x1, waiting for transfers between devices: 58.3 us -> 69.3 us  [shards(): lax.all_gather(wide_weight, ('seq', 'bucket'), axis=0, tiled=True)]
    slice x5 -> x1, local copies, waits for them, and re-layouts: 13.3 us -> 3.3 us  [shards(): value_rows[offset * row_count:(offset + 1) * row_count]]
    all_to_all x0 -> x2, starting transfers between devices: none -> 7.77 us  [the longest x1 4.23 us: shards(): lax.all_to_all(values[0], 'seq', split_axis=1, concat_axis=0, tiled=True)]
    all_gather x2 -> x1, waiting for transfers between devices: 98.6 us -> 92.4 us  [shards(): lax.all_gather(jnp.concatenate([local_k, local_v], axis=1), 'tensor', axi...]
    all_to_all x1, blocking collectives: 16.7 us -> 22.8 us  [shards(): lax.all_to_all(mixed, 'seq', split_axis=0, concat_axis=1, tiled=True)]
    slice x5 -> x0, local copies, waits for them, and re-layouts: 6.07 us -> none  [shards(): key_rows[offset * row_count:(offset + 1) * row_count]]
  transfers between devices with their start and end apart: 5 -> 6, of which waited for: 5 -> 6; matrix products, arithmetic and copies ran while one was open for 15% -> 9% of each run, Pallas kernels for 0% -> 0%
where the time goes in v1:
time: 300 us
  waiting for transfers between devices  214 us (71%)
  blocking collectives  22.8 us (8%)
  matrix products  17.3 us (6%)
  local copies, waits for them, and re-layouts  15.4 us (5%)
  between operations  14 us (5%)
  starting transfers between devices  11.4 us (4%)
  other arithmetic  4.87 us (2%)
    all_gather x1, waiting for transfers between devices, shards(): lax.all_gather(jnp.concatenate([local_k, local_v], axis=1), 'tensor', axi...  92.4 us
    all_gather x1, waiting for transfers between devices, shards(): lax.all_gather(wide_weight, ('seq', 'bucket'), axis=0, tiled=True)  69.3 us
    all_to_all x1, blocking collectives, shards(): lax.all_to_all(mixed, 'seq', split_axis=0, concat_axis=1, tiled=True)  22.8 us
    all_gather x1, waiting for transfers between devices, shards(): wide_weight = lax.all_gather(out_weight, 'tensor', axis=1, tiled=True)  20.7 us
    all_to_all x1, waiting for transfers between devices, shards(): lax.all_to_all(keys[0], 'seq', split_axis=1, concat_axis=0, tiled=True)  10.4 us
    all_to_all x1, waiting for transfers between devices, shards(): lax.all_to_all(values[0], 'seq', split_axis=1, concat_axis=0, tiled=True)  10.4 us
    all_to_all x1, waiting for transfers between devices, shards(): lax.all_to_all(queries[0], 'seq', split_axis=1, concat_axis=0, tiled=True)  10.2 us
    dot_general x1, matrix products, shards(): jnp.dot(restored, lax.all_gather(wide_weight, ('seq', 'bucket'), axis=0,...  9.87 us
  transfers between devices with their start and end apart: 6, of which 6 were waited for; matrix products, arithmetic and copies ran while one was open for 9% of the time, Pallas kernels for 0%

profile of v1, /device:TPU:0, one launch (start us, length us, event | category | flops | bytes accessed | tf_op | source)
XLA Modules:
  0.0 299.9 jit_solution(9476462355380110895)
XLA Ops:
  6.5 0.0 copy-start
  6.5 0.0 all-gather.6.cloned.1.call-start
  6.5 0.7 all-gather.6.cloned.1.call-update
  7.3 2.3 copy.30
  9.5 4.2 %all-to-all-start.1 = ((bf16[128,2,1536]{0,2,1:T(8,128)(2,1)}), bf16[128,2,1536]{0,2,1:T(8,128)(2,1)S(1)}, u32[]{:S(2)}, u32[]{:S(2)}) async-start(bf16[128,2,1536]{0,2,1:T(8,128)(2,1)} %bitcast.3), calls=%async_computation.1 | async-start | bytes 1572864 | tf_op jit(solution)/shard_map/all_to_all | solution.py:18
  13.8 0.0 copy-done
  13.8 1.2 copy.28
  14.9 10.4 %all-to-all-done.1 = bf16[128,2,1536]{0,2,1:T(8,128)(2,1)S(1)} async-done(((bf16[128,2,1536]{0,2,1:T(8,128)(2,1)}), bf16[128,2,1536]{0,2,1:T(8,128)(2,1)S(1)}, u32[]{:S(2)}, u32[]{:S(2)}) %all-to-all-start.1) | async-done | bytes 786464 | tf_op jit(solution)/shard_map/all_to_all | solution.py:18
  25.4 3.5 %all-to-all-start = ((bf16[128,2,1536]{0,2,1:T(8,128)(2,1)}), bf16[128,2,1536]{0,2,1:T(8,128)(2,1)S(1)}, u32[]{:S(2)}, u32[]{:S(2)}) async-start(bf16[128,2,1536]{0,2,1:T(8,128)(2,1)} %bitcast.1), calls=%async_computation | async-start | bytes 1572864 | tf_op jit(solution)/shard_map/all_to_all | solution.py:17
  28.9 0.0 all-gather.4.cloned.1.call-start
  29.0 0.1 copy_bitcast_fusion
  29.0 10.4 %all-to-all-done = bf16[128,2,1536]{0,2,1:T(8,128)(2,1)S(1)} async-done(((bf16[128,2,1536]{0,2,1:T(8,128)(2,1)}), bf16[128,2,1536]{0,2,1:T(8,128)(2,1)S(1)}, u32[]{:S(2)}, u32[]{:S(2)}) %all-to-all-start) | async-done | bytes 786464 | tf_op jit(solution)/shard_map/all_to_all | solution.py:17
  39.5 0.1 copy_bitcast_fusion.1
  39.6 0.0 copy-start.1
  39.6 1.2 pad_maximum_fusion
  40.8 0.0 all-gather.4.cloned.1.call-update
  40.9 0.0 all-gather.8.cloned.1.call-start
  40.9 20.7 %all-gather.6.cloned.1.call-done = bf16[384,3072]{1,0:T(8,128)(2,1)} async-done(((bf16[384,768]{1,0:T(8,128)(2,1)}), bf16[384,3072]{1,0:T(8,128)(2,1)}) %all-gather.6.cloned.1.call-update) | async-done | bytes 2359312 | tf_op jit(solution)/shard_map/all_gather | solution.py:72
  61.6 0.0 all-gather.8.cloned.1.call-update
  61.7 0.0 copy-done.1
  61.7 1.2 copy.32
  62.8 3.5 %all-to-all-start.2 = ((bf16[128,2,1536]{0,2,1:T(8,128)(2,1)}), bf16[128,2,1536]{0,2,1:T(8,128)(2,1)S(1)}, u32[]{:S(2)}, u32[]{:S(2)}) async-start(bf16[128,2,1536]{0,2,1:T(8,128)(2,1)} %bitcast.6), calls=%async_computation.2 | async-start | bytes 1572864 | tf_op jit(solution)/shard_map/all_to_all | solution.py:16
  67.1 10.2 %all-to-all-done.2 = bf16[128,2,1536]{0,2,1:T(8,128)(2,1)S(1)} async-done(((bf16[128,2,1536]{0,2,1:T(8,128)(2,1)}), bf16[128,2,1536]{0,2,1:T(8,128)(2,1)S(1)}, u32[]{:S(2)}, u32[]{:S(2)}) %all-to-all-start.2) | async-done | bytes 786464 | tf_op jit(solution)/shard_map/all_to_all | solution.py:16
  77.3 6.7 %copy.33 = bf16[2,128,1536]{1,0,2:T(2,128)(2,1)S(1)} copy(bf16[2,128,1536]{1,2,0:T(8,128)(2,1)S(1)} %bitcast.128) | data formatting | bytes 1572864 | tf_op jit(solution)/shard_map/all_to_all | solution.py:16
  83.9 0.5 reshape.424
  84.4 92.4 %all-gather.4.cloned.1.call-done = bf16[1024,3072]{0,1:T(8,128)(2,1)} async-done(((bf16[256,3072]{0,1:T(8,128)(2,1)}), bf16[1024,3072]{0,1:T(8,128)(2,1)}) %all-gather.4.cloned.1.call-update) | async-done | bytes 6291472 | tf_op jit(solution)/shard_map/all_gather | solution.py:39
  176.8 3.3 %fusion.89 = (bf16[256,1536]{0,1:T(8,128)(2,1)S(1)}, bf16[256,1536]{0,1:T(8,128)(2,1)S(1)}, bf16[256,1536]{0,1:T(8,128)(2,1)S(1)}, bf16[256,1536]{0,1:T(8,128)(2...) fusion(bf16[1024,3072]{0,1:T(8,128)(2,1)} %all-gather.4.cloned., ...), kind=kLoop, calls=%fused_computation.159 | loop fusion | bytes 12582912 | tf_op jit(solution)/shard_map/slice | solution.py:48
  180.1 0.9 bitcast_reduce_fusion.3
  181.0 0.9 bitcast_reduce_fusion
  181.9 0.8 bitcast_reduce_fusion.1
  182.7 0.9 bitcast_reduce_fusion.2
  183.6 0.8 fusion.11
  184.4 0.8 fusion.13
  185.3 0.8 fusion.15
  186.1 0.8 fusion.9
  187.0 0.9 fusion.21
  188.0 0.9 fusion.19
  188.9 0.9 fusion.17
  189.8 1.3 fusion.25
  191.1 0.2 reshape.432
  191.3 0.2 fusion.29
  191.5 22.8 %all_to_all.70 = bf16[2,128,1536]{1,2,0:T(8,128)(2,1)S(1)} all-to-all(bf16[2,128,1536]{1,2,0:T(8,128)(2,1)S(1)} %fusion.29), channel_id=1, replica_groups=mesh['seq'=2,'tensor'=4,'bucket'=4] {'seq'}, dimensions={0} | all-to-all | bytes 1572864 | tf_op jit(solution)/shard_map/all_to_all | solution.py:71
  214.2 69.3 %all-gather.8.cloned.1.call-done = bf16[3072,3072]{1,0:T(8,128)(2,1)} async-done(((bf16[384,3072]{1,0:T(8,128)(2,1)}), bf16[3072,3072]{1,0:T(8,128)(2,1)}) %all-gather.8.cloned.1.call-update) | async-done | bytes 18874384 | tf_op jit(solution)/shard_map/all_gather | solution.py:75
  283.5 9.9 %fusion = bf16[1,128,3072]{2,1,0:T(8,128)(2,1)} fusion(bf16[128,3072]{0,1:T(8,128)(2,1)S(1)} %bitcast.123, bf16[3072,3072]{1,0:T(8,128)(2,1)} %all-gather.8.cloned.1.call-done), kind=kOutput, calls=%fused_computation.1 | convolution fusion | flops 2416312320 | bytes 20447232 | tf_op jit(solution)/shard_map/dot_general | solution.py:73
  (5 shorter events, 0.1 us)
Async XLA Ops:
  6.5 7.2 %copy-start = (bf16[1,128,3072]{2,1,0:T(8,128)(2,1)S(1)}, bf16[1,128,3072]{2,1,0:T(8,128)(2,1)}, u32[]{:S(2)}) copy-start(bf16[1,128,3072]{2,1,0:T(8,128)(2,1)} %param.6) | copy-start | bytes 2359300
  6.5 55.1 %all-gather.6.cloned.1.call-start = ((), (), s32[]{:S(2)}) async-start(), calls=%async_computation.5 | async-start | bytes 2949120 | tf_op jit(solution)/shard_map/all_gather | solution.py:72
  9.5 15.8 %all-to-all-start.1 = ((bf16[128,2,1536]{0,2,1:T(8,128)(2,1)}), bf16[128,2,1536]{0,2,1:T(8,128)(2,1)S(1)}, u32[]{:S(2)}, u32[]{:S(2)}) async-start(bf16[128,2,1536]{0,2,1:T(8,128)(2,1)} %bitcast.3), calls=%async_computation.1 | async-start | bytes 1572864 | tf_op jit(solution)/shard_map/all_to_all | solution.py:18
  25.4 14.1 %all-to-all-start = ((bf16[128,2,1536]{0,2,1:T(8,128)(2,1)}), bf16[128,2,1536]{0,2,1:T(8,128)(2,1)S(1)}, u32[]{:S(2)}, u32[]{:S(2)}) async-start(bf16[128,2,1536]{0,2,1:T(8,128)(2,1)} %bitcast.1), calls=%async_computation | async-start | bytes 1572864 | tf_op jit(solution)/shard_map/all_to_all | solution.py:17
  28.9 147.9 %all-gather.4.cloned.1.call-start = ((), (), s32[]{:S(2)}) async-start(), calls=%async_computation.4 | async-start | bytes 7864320 | tf_op jit(solution)/shard_map/all_gather | solution.py:39
  39.6 22.1 %copy-start.1 = (bf16[1,128,3072]{2,1,0:T(8,128)(2,1)S(1)}, bf16[1,128,3072]{2,1,0:T(8,128)(2,1)}, u32[]{:S(2)}) copy-start(bf16[1,128,3072]{2,1,0:T(8,128)(2,1)} %param.5) | copy-start | bytes 2359300
  40.9 242.6 %all-gather.8.cloned.1.call-start = ((), (), s32[]{:S(2)}) async-start(), calls=%async_computation.6 | async-start | bytes 21233664 | tf_op jit(solution)/shard_map/all_gather | solution.py:75
  62.8 14.4 %all-to-all-start.2 = ((bf16[128,2,1536]{0,2,1:T(8,128)(2,1)}), bf16[128,2,1536]{0,2,1:T(8,128)(2,1)S(1)}, u32[]{:S(2)}, u32[]{:S(2)}) async-start(bf16[128,2,1536]{0,2,1:T(8,128)(2,1)} %bitcast.6), calls=%async_computation.2 | async-start | bytes 1572864 | tf_op jit(solution)/shard_map/all_to_all | solution.py:16
Sparse Core Ops, SparseCore 0:
  8.9 52.6 all-gather.5
  63.2 113.5 all-gather.3
  178.7 104.7 all-gather.7
